TPU v7x, 256 devices: a whole 4x4x8 slice. The times are simulated.
256 devices in a mesh: blk: 64 (over y, z, x_hi), tp: 4 (over x_lo, core).
Axes of the slice: x: 4 (x_hi: 2, x_lo: 2; x = x_hi * 2 + x_lo), y: 4, z: 8, core: 2. Of those that a mesh axis runs over, the one named last changes fastest.
Arguments:
- kv_keys: bfloat16 [256, 2048, 512], P('blk', None, 'tp'), may hold values from -6 to 6
- kv_values: bfloat16 [256, 2048, 512], P('blk', None, 'tp'), may hold values from -6 to 6
- queries: bfloat16 [256, 128, 3584], P('blk', None, 'tp'), may hold values from -170 to 170, as said below
- hidden: bfloat16 [256, 128, 3584], P('blk', None, 'tp'), may hold values from -2 to 2
- out_weight: bfloat16 [3584, 3584], P('tp'), may hold values from -0.09375 to 0.09375
- block_live: int32 [256], P('blk'), may hold values from 1 to 128
- node_tiles: int32 [256, 128], P('blk'), may hold values from 1 to 16
- left_count: int32 [64], P('blk'), may hold values from 1 to 2, as said below
- right_count: int32 [64], P('blk'), may hold values from 1 to 2, as said below
Outputs:
- balanced: bfloat16 [512, 128, 3584], P('blk', None, 'tp')
Inputs may be any that keep to these rules, and one draw needn't show every extreme that they name: `queries`: queries of the nodes. `left_count`: at most 2; some index reaches 2 in every draw. `right_count`: at most 2; some index reaches 2 in every draw.
All inputs are finite; a program needn't handle non-finite values.
Results may differ from a plain program's by a relative error of at most 0.0047.
Values may be sent and summed in bfloat16 or wider, within the bound.
A program may use at most 192 MiB of HBM per device.

v0:
```python
import jax
import jax.numpy as jnp
from jax import lax
from jax.sharding import PartitionSpec as P

TILE = 128
S_MAX = 2


def in_blocks(x, dim, peers):
    shape = x.shape
    parts = x.reshape(*shape[:dim], peers, shape[dim] // peers, *shape[dim + 1 :])
    return jnp.moveaxis(parts, dim, 0)


def sent_and_summed(x, axis, dim):
    peers = lax.axis_size(axis)
    parts = lax.all_to_all(in_blocks(x, dim, peers), axis, 0, 0, tiled=True)
    return jnp.sum(parts.astype(jnp.float32), axis=0)


def passed_along(value, axis, steps):
    count = lax.axis_size(axis)
    pairs = [(source, (source + steps) % count) for source in range(count)]
    return lax.ppermute(value, axis, pairs)


def attend(query_rows, key_rows, value_rows, tiles):
    batch_size, node_count, row_width = query_rows.shape
    head_size = key_rows.shape[2]
    group_size = row_width // head_size
    flat_rows = query_rows.reshape(batch_size, node_count * group_size, head_size)
    scores = jnp.einsum(
        "srd,spd->srp", flat_rows, key_rows, preferred_element_type=jnp.float32
    ) * head_size ** (-0.5)
    reach = jnp.repeat(tiles, group_size, axis=1) * TILE
    places = lax.broadcasted_iota(jnp.int32, (1, 1, key_rows.shape[1]), 2)
    inside = places < reach[:, :, None]
    scores = jnp.where(inside, scores, jnp.float32(-1e30))
    row_max = jnp.max(scores, axis=-1, keepdims=True)
    weights_exp = jnp.where(inside, jnp.exp(scores - row_max), jnp.float32(0.0))
    weights = (weights_exp / jnp.sum(weights_exp, axis=-1, keepdims=True)).astype(jnp.bfloat16)
    mixed = jnp.einsum("srp,spd->srd", weights, value_rows, preferred_element_type=jnp.float32)
    return mixed.astype(jnp.bfloat16).reshape(batch_size, node_count, row_width)


def finish(attn, residual, live_counts, out_weight):
    batch_size, node_count, row_width = attn.shape
    flat_attn = attn.reshape(batch_size * node_count, row_width)
    partial_value = jnp.dot(flat_attn, out_weight, preferred_element_type=jnp.float32)
    summed = sent_and_summed(partial_value.astype(jnp.bfloat16), "tp", 1)
    node_out = residual.astype(jnp.float32) + summed.reshape(residual.shape)
    node_live = jnp.arange(node_count, dtype=jnp.int32)[None, :] < live_counts[:, None]
    return jnp.where(node_live[:, :, None], node_out, jnp.float32(0.0))


def slot_usable(prev_right, own_left, own_right, next_left, block_count):
    slot_index = jnp.arange(block_count + 2 * S_MAX, dtype=jnp.int32)
    from_prev = slot_index < S_MAX
    from_next = slot_index >= S_MAX + block_count
    own_blk = slot_index - S_MAX
    own_usable = (own_blk >= own_left) & (own_blk < block_count - own_right)
    return jnp.where(
        from_prev,
        S_MAX - slot_index <= prev_right,
        jnp.where(from_next, slot_index - S_MAX - block_count < next_left, own_usable),
    )


def on_device(
    kv_keys, kv_values, queries, hidden, out_weight, block_live, node_tiles, left_count, right_count
):
    block_count = kv_keys.shape[0]
    attn = attend(queries, kv_keys, kv_values, node_tiles)
    node_out = finish(attn, hidden, block_live, out_weight).astype(jnp.bfloat16)
    from_prev = passed_along((node_out[block_count - S_MAX :], right_count), "blk", 1)
    from_next = passed_along((node_out[:S_MAX], left_count), "blk", -1)
    all_out = jnp.concatenate([from_prev[0], node_out, from_next[0]], axis=0)
    usable = slot_usable(
        from_prev[1][0], left_count[0], right_count[0], from_next[1][0], block_count
    )
    return jnp.where(usable[:, None, None], all_out, jnp.zeros((), jnp.bfloat16))


def solution(mesh):
    return jax.shard_map(
        on_device,
        mesh=mesh,
        in_specs=(
            P("blk", None, "tp"),
            P("blk", None, "tp"),
            P("blk", None, "tp"),
            P("blk", None, "tp"),
            P("tp", None),
            P("blk"),
            P("blk", None),
            P("blk"),
            P("blk"),
        ),
        out_specs=P("blk", None, "tp"),
        check_vma=False,
    )
```

profile of v0, /device:TPU:1, one launch (start us, length us, event | category | flops | bytes accessed | tf_op | source)
XLA Modules:
  0.0 187.8 jit_solution(12057196305983587089)
XLA Ops:
  0.0 0.0 copy-start
  0.0 2.1 %reshape.61 = bf16[4,896,128]{2,1,0:T(8,128)(2,1)S(1)} reshape(bf16[4,128,896]{2,1,0:T(8,128)(2,1)} %param.11) | data formatting | bytes 1835008 | tf_op jit(solution)/shard_map/reshape | solution.py:32
  2.2 0.7 broadcast_multiply_fusion
  2.8 0.1 broadcast_in_dim.43
  3.0 0.2 mul.22
  3.2 0.0 copy-done
  3.2 11.7 %fusion.17 = f32[4,896,2048]{2,1,0:T(8,128)} fusion(bf16[4,896,128]{2,1,0:T(8,128)(2,1)S(1)} %reshape.61, bf16[4,2048,128]{2,1,0:T(8,128)(2,1)S(1)} %copy-done), kind=kOutput, calls=%fused_computation.27 | convolution fusion | flops 1879048192 | bytes 32374784 | tf_op jit(solution)/shard_map/srd,spd->srp/dot_general | solution.py:33
  14.9 42.8 %fusion.16 = f32[4,896]{1,0:T(4,128)S(1)} fusion(f32[4,896,2048]{2,1,0:T(8,128)} %fusion.17, s32[4,896]{1,0:T(4,128)S(1)} %mul.22), kind=kOutput, calls=%fused_computation.26 | output fusion | flops 51382272 | bytes 29388800 | tf_op jit(solution)/shard_map/sub | solution.py:41
  57.7 40.3 %fusion.6 = bf16[4,896,128]{2,1,0:T(8,128)(2,1)S(1)} fusion(bf16[4,2048,128]{2,1,0:T(8,128)(2,1)} %param.10, f32[4,896]{1,0:T(4,128)S(1)} %fusion.16, f32[4,896,2048]{2,1,0:T(8,128)} %fusion.17, s32[4,896]{1,0:T(4,128)S(1)} %mul.22), kind=kOutput, calls=%fused_computation.15 | convolution fusion | flops 1938232832 | bytes 32403456 | tf_op jit(solution)/shard_map/srp,spd->srd/dot_general | solution.py:43
  98.0 1.8 reshape_reshape.3
  99.8 0.0 copy-start.2
  99.8 7.1 %convolution_convert_fusion = bf16[512,3584]{1,0:T(8,128)(2,1)S(1)} fusion(bf16[512,896]{1,0:T(8,128)(2,1)} %reshape_reshape.3, bf16[896,3584]{1,0:T(8,128)(2,1)} %param.13), kind=kOutput, calls=%fused_computation.11 | convolution fusion | flops 3290169344 | bytes 11010048 | tf_op jit(solution)/shard_map/dot_general | solution.py:50
  106.9 0.0 copy-start.1
  106.9 2.1 %copy.13 = bf16[64,4,8,896]{3,2,0,1:T(8,128)(2,1)} copy(bf16[64,4,8,896]{3,2,1,0:T(8,128)(2,1)S(1)} %bitcast.20) | data formatting | bytes 7340032 | tf_op jit(solution)/shard_map/reshape | solution.py:12
  109.1 7.9 %all-to-all-start = ((bf16[4,512,896]{2,1,0:T(8,128)(2,1)}), bf16[4,512,896]{2,1,0:T(8,128)(2,1)}, u32[]{:S(2)}, u32[]{:S(2)}) async-start(bf16[4,512,896]{2,1,0:T(8,128)(2,1)} %bitcast.18), calls=%async_computation | async-start | bytes 7340032 | tf_op jit(solution)/shard_map/all_to_all | solution.py:18
  117.0 0.0 copy-done.2
  117.0 0.1 iota_compare_fusion.1
  117.0 41.6 %all-to-all-done = bf16[4,512,896]{2,1,0:T(8,128)(2,1)} async-done(((bf16[4,512,896]{2,1,0:T(8,128)(2,1)}), bf16[4,512,896]{2,1,0:T(8,128)(2,1)}, u32[]{:S(2)}, u32[]{:S(2)}) %all-to-all-start) | async-done | bytes 3670048 | tf_op jit(solution)/shard_map/all_to_all | solution.py:18
  158.6 2.7 %convert_reduce_fusion = f32[512,896]{1,0:T(8,128)S(1)} fusion(bf16[4,512,896]{2,1,0:T(8,128)(2,1)} %all-to-all-done), kind=kLoop, calls=%fused_computation.10 | loop fusion | flops 3211264 | bytes 5505024 | tf_op jit(solution)/shard_map/reduce_sum | solution.py:19
  161.4 0.0 copy-done.1
  161.4 0.3 select_convert_fusion
  161.6 0.1 fusion.15
  161.7 1.1 collective-permute-start.2
  162.8 7.8 %collective-permute-start.3 = (bf16[2,128,896]{2,1,0:T(8,128)(2,1)S(1)}, bf16[2,128,896]{2,1,0:T(8,128)(2,1)S(1)}, u32[]{:S(2)}, u32[]{:S(2)}) collective-permute-start(bf16[2,128,896]{2,1,0:T(8,128)(2,1)S(1)} %get-tuple-element.6), channel_id=1, source_target_pairs={{0,252},{4,0},{8,4},{12,8},{16,12},{20,16},{24,20},{28,24},{32,28}... | collective-permute-start | bytes 1376264 | tf_op jit(solution)/shard_map/ppermute | solution.py:25
  170.7 0.0 collective-permute-start
  170.7 7.2 %collective-permute-start.1 = (s32[1]{0:T(128)}, s32[1]{0:T(128)}, u32[]{:S(2)}, u32[]{:S(2)}) collective-permute-start(s32[1]{0:T(128)} %param.16), channel_id=1, source_target_pairs={{0,252},{4,0},{8,4},{12,8},{16,12},{20,16},{24,20},{28,24},{32,28}... | collective-permute-start | bytes 20 | tf_op jit(solution)/shard_map/ppermute | solution.py:25
  179.2 2.5 %collective-permute-done = s32[1]{0:T(128)} collective-permute-done((s32[1]{0:T(128)}, s32[1]{0:T(128)}, u32[]{:S(2)}, u32[]{:S(2)}) %collective-permute-start) | collective-permute-done | bytes 36 | tf_op jit(solution)/shard_map/ppermute | solution.py:25
  181.6 3.4 %collective-permute-done.1 = s32[1]{0:T(128)} collective-permute-done((s32[1]{0:T(128)}, s32[1]{0:T(128)}, u32[]{:S(2)}, u32[]{:S(2)}) %collective-permute-start.1) | collective-permute-done | bytes 36 | tf_op jit(solution)/shard_map/ppermute | solution.py:25
  185.0 1.2 select_select_fusion
  186.2 0.0 collective-permute-done.2
  186.2 0.0 collective-permute-done.3
  186.2 1.6 maximum_select_fusion
Async XLA Ops:
  0.0 3.2 %copy-start = (bf16[4,2048,128]{2,1,0:T(8,128)(2,1)S(1)}, bf16[4,2048,128]{2,1,0:T(8,128)(2,1)}, u32[]{:S(2)}) copy-start(bf16[4,2048,128]{2,1,0:T(8,128)(2,1)} %param.9) | copy-start | bytes 6291460
  99.8 17.1 %copy-start.2 = (s32[4]{0:T(128)S(1)}, s32[4]{0:T(128)}, u32[]{:S(2)}) copy-start(s32[4]{0:T(128)} %param.14) | copy-start | bytes 52
  106.9 54.4 %copy-start.1 = (bf16[4,128,896]{2,1,0:T(8,128)(2,1)S(1)}, bf16[4,128,896]{2,1,0:T(8,128)(2,1)}, u32[]{:S(2)}) copy-start(bf16[4,128,896]{2,1,0:T(8,128)(2,1)} %param.12) | copy-start | bytes 2752516
  109.1 49.6 %all-to-all-start = ((bf16[4,512,896]{2,1,0:T(8,128)(2,1)}), bf16[4,512,896]{2,1,0:T(8,128)(2,1)}, u32[]{:S(2)}, u32[]{:S(2)}) async-start(bf16[4,512,896]{2,1,0:T(8,128)(2,1)} %bitcast.18), calls=%async_computation | async-start | bytes 7340032 | tf_op jit(solution)/shard_map/all_to_all | solution.py:18
  161.7 24.5 %collective-permute-start.2 = (bf16[2,128,896]{2,1,0:T(8,128)(2,1)S(1)}, bf16[2,128,896]{2,1,0:T(8,128)(2,1)S(1)}, u32[]{:S(2)}, u32[]{:S(2)}) collective-permute-start(bf16[2,128,896]{2,1,0:T(8,128)(2,1)S(1)} %get-tuple-element.5), channel_id=1, source_target_pairs={{0,4},{4,8},{8,12},{12,16},{16,20},{20,24},{24,28},{28,32},{32,36}... | collective-permute-start | bytes 1376264 | tf_op jit(solution)/shard_map/ppermute | solution.py:25
  162.8 23.4 %collective-permute-start.3 = (bf16[2,128,896]{2,1,0:T(8,128)(2,1)S(1)}, bf16[2,128,896]{2,1,0:T(8,128)(2,1)S(1)}, u32[]{:S(2)}, u32[]{:S(2)}) collective-permute-start(bf16[2,128,896]{2,1,0:T(8,128)(2,1)S(1)} %get-tuple-element.6), channel_id=1, source_target_pairs={{0,252},{4,0},{8,4},{12,8},{16,12},{20,16},{24,20},{28,24},{32,28}... | collective-permute-start | bytes 1376264 | tf_op jit(solution)/shard_map/ppermute | solution.py:25
  170.7 11.0 %collective-permute-start = (s32[1]{0:T(128)}, s32[1]{0:T(128)}, u32[]{:S(2)}, u32[]{:S(2)}) collective-permute-start(s32[1]{0:T(128)} %param.17), channel_id=1, source_target_pairs={{0,4},{4,8},{8,12},{12,16},{16,20},{20,24},{24,28},{28,32},{32,36}... | collective-permute-start | bytes 20 | tf_op jit(solution)/shard_map/ppermute | solution.py:25
  170.7 14.3 %collective-permute-start.1 = (s32[1]{0:T(128)}, s32[1]{0:T(128)}, u32[]{:S(2)}, u32[]{:S(2)}) collective-permute-start(s32[1]{0:T(128)} %param.16), channel_id=1, source_target_pairs={{0,252},{4,0},{8,4},{12,8},{16,12},{20,16},{24,20},{28,24},{32,28}... | collective-permute-start | bytes 20 | tf_op jit(solution)/shard_map/ppermute | solution.py:25
where the time goes:
time: 189 us; the launch traced here: 188 us
  matrix products  59.1 us (31%)
  other arithmetic  49.3 us (26%)
  waiting for transfers between devices  47.5 us (25%)
  starting transfers between devices  24 us (13%)
  local copies, waits for them, and re-layouts  6.54 us (3%)
    sub x1, other arithmetic, attend(): weights_exp = jnp.where(inside, jnp.exp(scores - row_max), jnp.float32(0.0))  42.8 us
    all_to_all x1, waiting for transfers between devices, sent_and_summed(): parts = lax.all_to_all(in_blocks(x, dim, peers), axis, 0, 0, tiled=True)  41.6 us
    dot_general x1, matrix products, attend(): jnp.einsum('srp,spd->srd', weights, value_rows, preferred_element_type=jn...  40.3 us
    ppermute x4, starting transfers between devices, passed_along(): return lax.ppermute(value, axis, pairs)  16.1 us
    dot_general x1, matrix products, attend(): jnp.einsum('srd,spd->srp', flat_rows, key_rows, preferred_element_type=jn...  11.7 us
    all_to_all x1, starting transfers between devices, sent_and_summed(): parts = lax.all_to_all(in_blocks(x, dim, peers), axis, 0, 0, tiled=True)  7.9 us
    dot_general x1, matrix products, finish(): jnp.dot(flat_attn, out_weight, preferred_element_type=jnp.float32)  7.08 us
    ppermute x4, waiting for transfers between devices, passed_along(): return lax.ppermute(value, axis, pairs)  5.87 us
  transfers between devices with their start and end apart: 5, of which 3 were waited for; matrix products, arithmetic and copies ran while one was open for 1% of the time, Pallas kernels for 0%

commit v1 on v0

v1 whole, which is shorter than its diff:
```python
import functools
import math

import jax
import jax.numpy as jnp
from jax import lax
from jax.experimental import pallas as pl
from jax.experimental.pallas import tpu as pltpu
from jax.sharding import PartitionSpec as P

TILE = 128
HEAD = 128
S_MAX = 2
MASKED = -(2.0**100)
MESH = pl.DeviceIdType.MESH
ORDER = (0, 3, 1, 2)
GROUPS = ((0, 2), (2, 4), (4, 6), (6, 7))
PIECES = ((0, 512), (512, 896))
CHUNK = 512


def block_kernel(
    live_ref, left_ref, right_ref, tiles_ref, k_hbm, v_hbm, q_hbm, hid_hbm, w_hbm,
    out_ref,
    kb, vb, qb, hb, wb, ind, ones, far, sc, pr, ab, keep, snd, rcv, cut,
    k_sem, v_sem, q_sem, h_sem, w_sem, ws_sem, wr_sem, as_sem, ar_sem,
    is_sem, ir_sem, cs_sem, cr_sem,
    *, ring,
):
    blocks, tokens, _ = kb.shape
    nodes, width = qb.shape[1:]
    b = lax.axis_index("blk")
    t = lax.axis_index("tp")
    half = t // 2
    core = t % 2
    prev = (b + ring - 1) % ring
    following = (b + 1) % ring
    partner = (b, 2 * half + 1 - core)
    across = 2 * (1 - half) + core
    peer = (b, across)

    barrier = pltpu.get_barrier_semaphore()
    for other in (partner, peer, (prev, across), (following, across)):
        pl.semaphore_signal(barrier, inc=1, device_id=other, device_id_type=MESH)

    def local(src, dst, sem):
        return pltpu.make_async_copy(src, dst, sem)

    def remote(src, dst, send, recv, device):
        return pltpu.make_async_remote_copy(
            src_ref=src, dst_ref=dst, send_sem=send, recv_sem=recv,
            device_id=device, device_id_type=MESH,
        )

    def columns(quarter):
        return pl.ds(pl.multiple_of(quarter * width, width), width)

    def load_block(j):
        return (
            local(q_hbm.at[j], qb.at[j], q_sem.at[j]),
            local(k_hbm.at[j], kb.at[j], k_sem.at[j]),
            local(v_hbm.at[j], vb.at[j], v_sem.at[j]),
        )

    near_w = [
        local(w_hbm.at[:, columns(2 * h + core)], wb.at[h, pl.ds(0, width)], w_sem.at[n])
        for n, h in enumerate((half, 1 - half))
    ]
    far_w = [
        remote(
            w_hbm.at[:, columns(2 * h + 1 - core)], wb.at[h, pl.ds(width, width)],
            ws_sem.at[n], wr_sem.at[n], partner,
        )
        for n, h in enumerate((half, 1 - half))
    ]
    hid_copy = local(hid_hbm, hb, h_sem)

    for copy in load_block(ORDER[0]):
        copy.start()

    token = lax.broadcasted_iota(jnp.int32, (tokens, HEAD), 0)
    lane = lax.broadcasted_iota(jnp.int32, (tokens, HEAD), 1)
    ind[...] = jnp.where(token // TILE == lane, 1.0, 0.0).astype(jnp.bfloat16)
    ones[...] = jnp.ones_like(ones)
    node_lane = lax.broadcasted_iota(jnp.int32, (nodes, HEAD), 1).astype(jnp.float32)
    for j in range(blocks):
        row = tiles_ref[pl.ds(j, 1), :].astype(jnp.float32)
        reach = jnp.transpose(jnp.broadcast_to(row, (HEAD, nodes)))
        far[j] = jnp.where(node_lane < reach, 0.0, MASKED).astype(jnp.bfloat16)
    zero_rows = jnp.zeros((nodes, width), jnp.bfloat16)
    out_ref[S_MAX] = zero_rows
    out_ref[S_MAX + blocks - 1] = zero_rows

    pl.semaphore_wait(barrier, 4)
    far_w[0].start()
    near_w[0].start()
    for j in ORDER[1:2]:
        for copy in load_block(j):
            copy.start()
    far_w[1].start()
    near_w[1].start()
    hid_copy.start()
    for j in ORDER[2:]:
        for copy in load_block(j):
            copy.start()

    scale = jnp.float32(HEAD**-0.5 * math.log2(math.e))
    attn_copies = {
        j: remote(
            ab.at[j, :, pl.ds(0, width)], ab.at[j, :, pl.ds(width, width)],
            as_sem.at[j], ar_sem.at[j], partner,
        )
        for j in range(blocks)
    }
    inner = {
        (j, n): remote(
            snd.at[j, :, pl.ds(lo, hi - lo)], rcv.at[j, :, pl.ds(lo, hi - lo)],
            is_sem.at[j, n], ir_sem.at[j, n], peer,
        )
        for j in range(blocks)
        for n, (lo, hi) in enumerate(PIECES)
    }
    outer = {
        (j, n): remote(
            cut.at[j, :, pl.ds(lo, hi - lo)],
            out_ref.at[(j + S_MAX + blocks) % (2 * blocks), :, pl.ds(lo, hi - lo)]
            if j < S_MAX
            else out_ref.at[j - S_MAX, :, pl.ds(lo, hi - lo)],
            cs_sem.at[j, n], cr_sem.at[j, n],
            (prev if j < S_MAX else following, across),
        )
        for j in range(blocks)
        for n, (lo, hi) in enumerate(PIECES)
    }
    moved = [
        jnp.int32(1),
        (left_ref[0] >= 2).astype(jnp.int32),
        (right_ref[0] >= 2).astype(jnp.int32),
        jnp.int32(1),
    ]

    def scores(j, g, slot):
        lo, hi = GROUPS[g]
        rows = (hi - lo) * nodes
        q_rows = jnp.concatenate(
            [qb[j, :, h * HEAD : (h + 1) * HEAD] for h in range(lo, hi)], axis=0
        )
        far_rows = jnp.concatenate([far[j]] * (hi - lo), axis=0)
        lhs = jnp.concatenate([q_rows, far_rows], axis=1)
        top = jnp.full((rows, HEAD), -jnp.inf, jnp.float32)
        for c in range(0, tokens, CHUNK):
            rhs = jnp.concatenate([kb[j, c : c + CHUNK, :], ind[c : c + CHUNK, :]], axis=1)
            part = lax.dot_general(
                lhs, rhs, (((1,), (1,)), ((), ())), preferred_element_type=jnp.float32
            )
            sc[slot, :rows, c : c + CHUNK] = part
            for w in range(0, CHUNK, HEAD):
                top = jnp.maximum(top, part[:, w : w + HEAD])
        return jnp.max(top, axis=1, keepdims=True)

    def mix(j, g, slot, top):
        lo, hi = GROUPS[g]
        rows = (hi - lo) * nodes
        total = None
        for c in range(0, tokens, CHUNK):
            part = jnp.exp2((sc[slot, :rows, c : c + CHUNK] - top) * scale).astype(jnp.bfloat16)
            rhs = jnp.concatenate([vb[j, c : c + CHUNK, :], ones[c : c + CHUNK, :]], axis=1)
            term = jnp.dot(part, rhs, preferred_element_type=jnp.float32)
            total = term if total is None else total + term
        mean = (total[:, :HEAD] / total[:, HEAD:]).astype(jnp.bfloat16)
        for n, h in enumerate(range(lo, hi)):
            ab[j, :, h * HEAD : (h + 1) * HEAD] = mean[n * nodes : (n + 1) * nodes]

    def attend(j):
        for copy in load_block(j):
            copy.wait()
        top = scores(j, 0, 0)
        for g in range(len(GROUPS)):
            ahead = scores(j, g + 1, (g + 1) % 2) if g + 1 < len(GROUPS) else None
            mix(j, g, g % 2, top)
            top = ahead

    def project(j):
        h_send = half * moved[j] + (1 - half) * (1 - moved[j])
        rows = ab[j]
        keeps = moved[j] == 0
        for n, (lo, hi) in enumerate(PIECES):
            part = jnp.dot(rows, wb[h_send, :, lo:hi], preferred_element_type=jnp.float32)
            residual = jnp.where(keeps, 0.0, hb[j, :, lo:hi].astype(jnp.float32))
            snd[j, :, lo:hi] = (part + residual).astype(jnp.bfloat16)
            inner[j, n].start()
        for n, (lo, hi) in enumerate(PIECES):
            part = jnp.dot(rows, wb[1 - h_send, :, lo:hi], preferred_element_type=jnp.float32)
            residual = jnp.where(keeps, hb[j, :, lo:hi].astype(jnp.float32), 0.0)
            keep[j, :, lo:hi] = part + residual

    def settle(j):
        for n, (lo, hi) in enumerate(PIECES):
            inner[j, n].wait_recv()
            total = keep[j, :, lo:hi] + rcv[j, :, lo:hi].astype(jnp.float32)
            node = lax.broadcasted_iota(jnp.int32, total.shape, 0)
            cut[j, :, lo:hi] = jnp.where(
                node < live_ref[j] * moved[j], total, 0.0
            ).astype(jnp.bfloat16)
            outer[j, n].start()
            if 0 < j < blocks - 1:
                out_ref[S_MAX + j, :, lo:hi] = jnp.where(
                    node < live_ref[j] * (1 - moved[j]), total, 0.0
                ).astype(jnp.bfloat16)

    def exchange(j, first):
        attn_copies[j].start()
        attn_copies[j].wait()
        if first:
            for copy in far_w + near_w:
                copy.wait()
            hid_copy.wait()

    for n, j in enumerate(ORDER):
        attend(j)
        exchange(j, n == 0)
        project(j)
        if n >= 2:
            settle(ORDER[n - 2])
    for j in ORDER[blocks - 2 :]:
        settle(j)
    for j in range(blocks):
        for n in range(len(PIECES)):
            inner[j, n].wait_send()
            outer[j, n].wait()


def on_device(kv_keys, kv_values, queries, hidden, out_weight, block_live, node_tiles, left_count, right_count, *, ring):
    blocks, tokens, _ = kv_keys.shape
    nodes, width = queries.shape[1:]
    hbm = pl.BlockSpec(memory_space=pltpu.MemorySpace.HBM)
    smem = pl.BlockSpec(memory_space=pltpu.MemorySpace.SMEM)
    vmem = pl.BlockSpec(memory_space=pltpu.MemorySpace.VMEM)
    rows = max(hi - lo for lo, hi in GROUPS) * nodes
    bf16, f32 = jnp.bfloat16, jnp.float32
    dma = pltpu.SemaphoreType.DMA
    pieces = len(PIECES)
    return pl.pallas_call(
        functools.partial(block_kernel, ring=ring),
        out_shape=jax.ShapeDtypeStruct((blocks + 2 * S_MAX, nodes, width), bf16),
        in_specs=[smem, smem, smem, vmem, hbm, hbm, hbm, hbm, hbm],
        out_specs=vmem,
        scratch_shapes=[
            pltpu.VMEM((blocks, tokens, HEAD), bf16),
            pltpu.VMEM((blocks, tokens, HEAD), bf16),
            pltpu.VMEM((blocks, nodes, width), bf16),
            pltpu.VMEM((blocks, nodes, width), bf16),
            pltpu.VMEM((2, 2 * width, width), bf16),
            pltpu.VMEM((tokens, HEAD), bf16),
            pltpu.VMEM((tokens, HEAD), bf16),
            pltpu.VMEM((blocks, nodes, HEAD), bf16),
            pltpu.VMEM((2, rows, tokens), f32),
            pltpu.VMEM((8, 128), bf16),
            pltpu.VMEM((blocks, nodes, 2 * width), bf16),
            pltpu.VMEM((blocks, nodes, width), f32),
            pltpu.VMEM((blocks, nodes, width), bf16),
            pltpu.VMEM((blocks, nodes, width), bf16),
            pltpu.VMEM((blocks, nodes, width), bf16),
            dma((blocks,)), dma((blocks,)), dma((blocks,)), dma, dma((2,)),
            dma((2,)), dma((2,)), dma((blocks,)), dma((blocks,)),
            dma((blocks, pieces)), dma((blocks, pieces)),
            dma((blocks, pieces)), dma((blocks, pieces)),
        ],
        compiler_params=pltpu.CompilerParams(
            collective_id=0, has_side_effects=True, vmem_limit_bytes=56 * 2**20
        ),
        name="rebalanced_attention",
    )(block_live, left_count, right_count, node_tiles, kv_keys, kv_values, queries, hidden, out_weight)


def solution(mesh):
    return jax.shard_map(
        functools.partial(on_device, ring=mesh.shape["blk"]),
        mesh=mesh,
        in_specs=(
            P("blk", None, "tp"),
            P("blk", None, "tp"),
            P("blk", None, "tp"),
            P("blk", None, "tp"),
            P("tp", None),
            P("blk"),
            P("blk", None),
            P("blk"),
            P("blk"),
        ),
        out_specs=P("blk", None, "tp"),
        check_vma=False,
    )
```

time: 189 us -> 55.1 us (0.29)
  matrix products: 59.1 us -> 0 us
  Pallas kernels: 0 us -> 50.3 us
  other arithmetic: 49.3 us -> 0 us
  waiting for transfers between devices: 47.5 us -> 0 us
  starting transfers between devices: 24 us -> 0 us
  local copies, waits for them, and re-layouts: 6.54 us -> 2.88 us
    dot_general x3 -> x0, matrix products: 59.1 us -> none  [the longest x1 40.3 us: attend(): jnp.einsum('srp,spd->srd', weights, value_rows, preferred_element_type=jn...]
    pallas_call x0 -> x1, Pallas kernels: none -> 50.3 us  [on_device(): pl.pallas_call(functools.partial(block_kernel, ring=ring), out_shape=jax....]
    sub x1 -> x0, other arithmetic: 42.8 us -> none  [attend(): weights_exp = jnp.where(inside, jnp.exp(scores - row_max), jnp.float32(0.0))]
    all_to_all x1 -> x0, waiting for transfers between devices: 41.6 us -> none  [sent_and_summed(): parts = lax.all_to_all(in_blocks(x, dim, peers), axis, 0, 0, tiled=True)]
    ppermute x4 -> x0, starting transfers between devices: 16.1 us -> none  [passed_along(): return lax.ppermute(value, axis, pairs)]
    all_to_all x1 -> x0, starting transfers between devices: 7.9 us -> none  [sent_and_summed(): parts = lax.all_to_all(in_blocks(x, dim, peers), axis, 0, 0, tiled=True)]
    ppermute x4 -> x0, waiting for transfers between devices: 5.87 us -> none  [passed_along(): return lax.ppermute(value, axis, pairs)]
    reshape x2 -> x0, local copies, waits for them, and re-layouts: 4.28 us -> none  [the longest x1 2.15 us: attend(): query_rows.reshape(batch_size, node_count * group_size, head_size)]
  transfers between devices with their start and end apart: 5 -> 0, of which waited for: 3 -> 0; matrix products, arithmetic and copies ran while one was open for 1% -> 0% of each run, Pallas kernels for 0% -> 0%
where the time goes in v1:
time: 55.1 us; the launch traced here: 54.5 us
  Pallas kernels  50.3 us (91%)
  local copies, waits for them, and re-layouts  2.88 us (5%)
  between operations  1.31 us (2%)
    pallas_call x1, Pallas kernels, on_device(): pl.pallas_call(functools.partial(block_kernel, ring=ring), out_shape=jax....  50.3 us
    unnamed x1, local copies, waits for them, and re-layouts  2.88 us

profile of v1, /device:TPU:1, one launch (start us, length us, event | category | flops | bytes accessed | tf_op | source)
XLA Modules:
  0.0 54.5 jit_solution(16531398073482164316)
XLA Ops:
  1.3 50.3 %rebalanced_attention.1 = bf16[8,128,896]{2,1,0:T(8,128)(2,1)} custom-call(s32[4]{0:T(128)} %live_ref.1, s32[1]{0:T(128)S(6)} %copy.11.left_ref, s32[1]{0:T(128)S(6)} %copy.12.right_ref, s32[4,128]{1,0:T(4,128)} %tiles_ref.1, bf16[4,2048,128]{2,1,0:T(8,128)(2,1)} %k_hbm.1, bf16[4,2048,128]{2,1,0:T(8,128)(2,1)} %v_hbm.1, bf16[4,128,896]{2,1,0:T(8,128)(2,1)} %q_hbm.1, ...), custom_call_target="tpu_custom_call" | custom-call | tf_op jit(solution)/shard_map/rebalanced_attention/pallas_call | solution.py:243
  51.6 2.9 %copy.13 = bf16[8,128,896]{2,1,0:T(8,128)(2,1)} copy(bf16[8,128,896]{2,1,0:T(8,128)(2,1)} %rebalanced_attention.1) | data formatting | bytes 3670016

commit v2 on v1

v2 whole, which is shorter than its diff:
```python
import functools
import math

import jax
import jax.numpy as jnp
from jax import lax
from jax.experimental import pallas as pl
from jax.experimental.pallas import tpu as pltpu
from jax.sharding import PartitionSpec as P

TILE = 128
HEAD = 128
S_MAX = 2
MASKED = -(2.0**100)
MESH = pl.DeviceIdType.MESH
ORDER = (0, 3, 1, 2)
GROUPS = ((0, 2), (2, 4), (4, 6), (6, 7))
PIECES = ((0, 256), (256, 512), (512, 896))
LAST_PIECES = ((0, 256), (256, 512), (512, 768), (768, 896))
CHUNK = 512


def pieces_of(j):
    return LAST_PIECES if j == ORDER[-1] else PIECES


def block_kernel(
    live_hbm, left_hbm, right_hbm, tiles_hbm, k_hbm, v_hbm, q_hbm, hid_hbm, w_hbm,
    out_ref,
    live_ref, left_ref, right_ref, tiles_ref,
    kb, vb, qb, hb, wb, ind, ones, far, sc, ab, keep, snd, rcv, cut,
    s_sem, k_sem, v_sem, q_sem, h_sem, w_sem, ws_sem, wr_sem, as_sem, ar_sem,
    is_sem, ir_sem, cs_sem, cr_sem,
    *, ring,
):
    blocks, tokens, _ = kb.shape
    nodes, width = qb.shape[1:]
    b = lax.axis_index("blk")
    t = lax.axis_index("tp")
    half = t // 2
    core = t % 2
    prev = (b + ring - 1) % ring
    following = (b + 1) % ring
    partner = (b, 2 * half + 1 - core)
    across = 2 * (1 - half) + core
    peer = (b, across)

    barrier = pltpu.get_barrier_semaphore()
    for other in (partner, peer, (prev, across), (following, across)):
        pl.semaphore_signal(barrier, inc=1, device_id=other, device_id_type=MESH)

    def local(src, dst, sem):
        return pltpu.make_async_copy(src, dst, sem)

    def remote(src, dst, send, recv, device):
        return pltpu.make_async_remote_copy(
            src_ref=src, dst_ref=dst, send_sem=send, recv_sem=recv,
            device_id=device, device_id_type=MESH,
        )

    q_copies = [local(q_hbm.at[j], qb.at[j], q_sem.at[j]) for j in range(blocks)]
    k_copies = [local(k_hbm.at[j], kb.at[j], k_sem.at[j]) for j in range(blocks)]
    v_copies = [local(v_hbm.at[j], vb.at[j], v_sem.at[j]) for j in range(blocks)]
    small = [
        local(tiles_hbm, tiles_ref, s_sem.at[0]),
        local(live_hbm, live_ref, s_sem.at[1]),
        local(left_hbm, left_ref, s_sem.at[2]),
        local(right_hbm, right_ref, s_sem.at[3]),
    ]
    hid_copy = local(hid_hbm, hb, h_sem)

    weight_parts = [(half, lo, hi) for lo, hi in PIECES] + [(1 - half, 0, width)]

    def weight_from(quarter, lo, hi):
        return w_hbm.at[:, pl.ds(pl.multiple_of(quarter * width + lo, HEAD), hi - lo)]

    near_w = [
        local(
            weight_from(2 * h + core, lo, hi),
            wb.at[h, pl.ds(0, width), pl.ds(lo, hi - lo)], w_sem.at[n],
        )
        for n, (h, lo, hi) in enumerate(weight_parts)
    ]
    far_w = [
        remote(
            weight_from(2 * h + 1 - core, lo, hi),
            wb.at[h, pl.ds(width, width), pl.ds(lo, hi - lo)],
            ws_sem.at[n], wr_sem.at[n], partner,
        )
        for n, (h, lo, hi) in enumerate(weight_parts)
    ]

    for copy in small[:1] + [q_copies[ORDER[0]], k_copies[ORDER[0]], v_copies[ORDER[0]]] + small[1:]:
        copy.start()
    for copy in near_w[:-1]:
        copy.start()
    q_copies[ORDER[1]].start()
    k_copies[ORDER[1]].start()
    v_copies[ORDER[1]].start()

    token = lax.broadcasted_iota(jnp.int32, (tokens, HEAD), 0)
    lane = lax.broadcasted_iota(jnp.int32, (tokens, HEAD), 1)
    ind[...] = jnp.where(token // TILE == lane, 1.0, 0.0).astype(jnp.bfloat16)
    ones[...] = jnp.ones_like(ones)
    zero_rows = jnp.zeros((nodes, width), jnp.bfloat16)
    out_ref[S_MAX] = zero_rows
    out_ref[S_MAX + blocks - 1] = zero_rows
    small[0].wait()
    node_lane = lax.broadcasted_iota(jnp.int32, (nodes, HEAD), 1).astype(jnp.float32)
    for j in range(blocks):
        row = tiles_ref[pl.ds(j, 1), :].astype(jnp.float32)
        reach = jnp.transpose(jnp.broadcast_to(row, (HEAD, nodes)))
        far[j] = jnp.where(node_lane < reach, 0.0, MASKED).astype(jnp.bfloat16)

    def enter():
        pl.semaphore_wait(barrier, 4)
        for copy in far_w[:-1]:
            copy.start()

    scale = jnp.float32(HEAD**-0.5 * math.log2(math.e))
    attn_copies = [
        remote(
            ab.at[j, :, pl.ds(0, width)], ab.at[j, :, pl.ds(width, width)],
            as_sem.at[j], ar_sem.at[j], partner,
        )
        for j in range(blocks)
    ]
    inner = {
        (j, n): remote(
            snd.at[j, :, pl.ds(lo, hi - lo)], rcv.at[j, :, pl.ds(lo, hi - lo)],
            is_sem.at[j, n], ir_sem.at[j, n], peer,
        )
        for j in range(blocks)
        for n, (lo, hi) in enumerate(pieces_of(j))
    }
    outer = {
        (j, n): remote(
            cut.at[j, :, pl.ds(lo, hi - lo)],
            out_ref.at[j + S_MAX + blocks if j < S_MAX else j - S_MAX, :, pl.ds(lo, hi - lo)],
            cs_sem.at[j, n], cr_sem.at[j, n],
            (prev if j < S_MAX else following, across),
        )
        for j in range(blocks)
        for n, (lo, hi) in enumerate(pieces_of(j))
    }

    def moved(j):
        if j == 1:
            return (left_ref[0] >= 2).astype(jnp.int32)
        if j == 2:
            return (right_ref[0] >= 2).astype(jnp.int32)
        return None

    def scores(j, g, slot):
        lo, hi = GROUPS[g]
        rows = (hi - lo) * nodes
        if g == 0:
            q_copies[j].wait()
            k_copies[j].wait()
        q_rows = jnp.concatenate(
            [qb[j, :, h * HEAD : (h + 1) * HEAD] for h in range(lo, hi)], axis=0
        )
        far_rows = jnp.concatenate([far[j]] * (hi - lo), axis=0)
        lhs = jnp.concatenate([q_rows, far_rows], axis=1)
        top = jnp.full((rows, HEAD), -jnp.inf, jnp.float32)
        for c in range(0, tokens, CHUNK):
            rhs = jnp.concatenate([kb[j, c : c + CHUNK, :], ind[c : c + CHUNK, :]], axis=1)
            part = lax.dot_general(
                lhs, rhs, (((1,), (1,)), ((), ())), preferred_element_type=jnp.float32
            )
            sc[slot, :rows, c : c + CHUNK] = part
            for w in range(0, CHUNK, HEAD):
                top = jnp.maximum(top, part[:, w : w + HEAD])
        return jnp.max(top, axis=1, keepdims=True)

    def mix(j, g, slot, top):
        lo, hi = GROUPS[g]
        rows = (hi - lo) * nodes
        if g == 0:
            v_copies[j].wait()
        total = None
        for c in range(0, tokens, CHUNK):
            part = jnp.exp2((sc[slot, :rows, c : c + CHUNK] - top) * scale).astype(jnp.bfloat16)
            rhs = jnp.concatenate([vb[j, c : c + CHUNK, :], ones[c : c + CHUNK, :]], axis=1)
            term = jnp.dot(part, rhs, preferred_element_type=jnp.float32)
            total = term if total is None else total + term
        mean = (total[:, :HEAD] / total[:, HEAD:]).astype(jnp.bfloat16)
        for n, h in enumerate(range(lo, hi)):
            ab[j, :, h * HEAD : (h + 1) * HEAD] = mean[n * nodes : (n + 1) * nodes]

    def residual(j, lo, hi, flag):
        rows = hb[j, :, lo:hi].astype(jnp.float32)
        return rows if flag is None else jnp.where(flag, rows, 0.0)

    def send_part(n):
        j = ORDER[n]
        attn_copies[j].wait()
        move = moved(j)
        pick = half if move is None else half * move + (1 - half) * (1 - move)
        for p, (lo, hi) in enumerate(pieces_of(j)):
            if n == 0:
                near_w[p].wait()
                far_w[p].wait()
            part = jnp.dot(ab[j], wb[pick, :, lo:hi], preferred_element_type=jnp.float32)
            if n == 0 and p == 0:
                hid_copy.wait()
            part = part + residual(j, lo, hi, None if move is None else move == 1)
            snd[j, :, lo:hi] = part.astype(jnp.bfloat16)
            inner[j, p].start()

    def keep_part(n):
        j = ORDER[n]
        move = moved(j)
        if n == 0:
            near_w[-1].wait()
            far_w[-1].wait()
        pick = 1 - half if move is None else half * (1 - move) + (1 - half) * move
        for lo, hi in pieces_of(j):
            part = jnp.dot(ab[j], wb[pick, :, lo:hi], preferred_element_type=jnp.float32)
            if move is not None:
                part = part + residual(j, lo, hi, move == 0)
            keep[j, :, lo:hi] = part

    def settle(n, p):
        j = ORDER[n]
        lo, hi = pieces_of(j)[p]
        move = moved(j)
        inner[j, p].wait_recv()
        total = keep[j, :, lo:hi] + rcv[j, :, lo:hi].astype(jnp.float32)
        node = lax.broadcasted_iota(jnp.int32, total.shape, 0)
        live = live_ref[j]
        leaving = live if move is None else live * move
        cut[j, :, lo:hi] = jnp.where(node < leaving, total, 0.0).astype(jnp.bfloat16)
        outer[j, p].start()
        if move is not None:
            out_ref[S_MAX + j, :, lo:hi] = jnp.where(
                node < live * (1 - move), total, 0.0
            ).astype(jnp.bfloat16)

    def pass_on(n):
        attn_copies[ORDER[n]].start()
        if n == 0:
            far_w[-1].start()

    groups = len(GROUPS)
    units = [(j, g) for j in ORDER for g in range(groups)]
    plan = {
        0: [(enter,)],
        3: [(pass_on, 0)],
        4: [(send_part, 0)],
        7: [(pass_on, 1), (keep_part, 0), (settle, 0, 0)],
        8: [(settle, 0, 1), (send_part, 1)],
        9: [(keep_part, 1), (settle, 0, 2)],
        11: [(pass_on, 2), (settle, 1, 0)],
        12: [(settle, 1, 1), (send_part, 2)],
        13: [(keep_part, 2), (settle, 1, 2)],
        15: [(pass_on, 3), (settle, 2, 0), (send_part, 3), (settle, 2, 1), (keep_part, 3),
             (settle, 2, 2)] + [(settle, 3, p) for p in range(len(LAST_PIECES))],
    }
    for copy in small[1:]:
        copy.wait()
    top = scores(*units[0], 0)
    hid_copy.start()
    near_w[-1].start()
    for j in ORDER[2:]:
        q_copies[j].start()
        k_copies[j].start()
        v_copies[j].start()
    for u, (j, g) in enumerate(units):
        ahead = scores(*units[u + 1], (u + 1) % 2) if u + 1 < len(units) else None
        mix(j, g, u % 2, top)
        top = ahead
        for step, *rest in plan.get(u, ()):
            step(*rest)
    for j in range(blocks):
        for n in range(len(pieces_of(j))):
            inner[j, n].wait_send()
            outer[j, n].wait()


def on_device(kv_keys, kv_values, queries, hidden, out_weight, block_live, node_tiles, left_count, right_count, *, ring):
    blocks, tokens, _ = kv_keys.shape
    nodes, width = queries.shape[1:]
    hbm = pl.BlockSpec(memory_space=pltpu.MemorySpace.HBM)
    vmem = pl.BlockSpec(memory_space=pltpu.MemorySpace.VMEM)
    rows = max(hi - lo for lo, hi in GROUPS) * nodes
    bf16, f32 = jnp.bfloat16, jnp.float32
    dma = pltpu.SemaphoreType.DMA
    pieces = max(len(PIECES), len(LAST_PIECES))
    parts = len(PIECES) + 1
    return pl.pallas_call(
        functools.partial(block_kernel, ring=ring),
        out_shape=pltpu.VMEM((blocks + 2 * S_MAX, nodes, width), bf16),
        in_specs=[hbm] * 9,
        out_specs=vmem,
        scratch_shapes=[
            pltpu.SMEM(block_live.shape, jnp.int32),
            pltpu.SMEM(left_count.shape, jnp.int32),
            pltpu.SMEM(right_count.shape, jnp.int32),
            pltpu.VMEM(node_tiles.shape, jnp.int32),
            pltpu.VMEM((blocks, tokens, HEAD), bf16),
            pltpu.VMEM((blocks, tokens, HEAD), bf16),
            pltpu.VMEM((blocks, nodes, width), bf16),
            pltpu.VMEM((blocks, nodes, width), bf16),
            pltpu.VMEM((2, 2 * width, width), bf16),
            pltpu.VMEM((tokens, HEAD), bf16),
            pltpu.VMEM((tokens, HEAD), bf16),
            pltpu.VMEM((blocks, nodes, HEAD), bf16),
            pltpu.VMEM((2, rows, tokens), f32),
            pltpu.VMEM((blocks, nodes, 2 * width), bf16),
            pltpu.VMEM((blocks, nodes, width), f32),
            pltpu.VMEM((blocks, nodes, width), bf16),
            pltpu.VMEM((blocks, nodes, width), bf16),
            pltpu.VMEM((blocks, nodes, width), bf16),
            dma((4,)), dma((blocks,)), dma((blocks,)), dma((blocks,)), dma, dma((parts,)),
            dma((parts,)), dma((parts,)), dma((blocks,)), dma((blocks,)),
            dma((blocks, pieces)), dma((blocks, pieces)),
            dma((blocks, pieces)), dma((blocks, pieces)),
        ],
        compiler_params=pltpu.CompilerParams(
            collective_id=0, has_side_effects=True, vmem_limit_bytes=56 * 2**20
        ),
        name="rebalanced_attention",
    )(block_live, left_count, right_count, node_tiles, kv_keys, kv_values, queries, hidden, out_weight)


def solution(mesh):
    return jax.shard_map(
        functools.partial(on_device, ring=mesh.shape["blk"]),
        mesh=mesh,
        in_specs=(
            P("blk", None, "tp"),
            P("blk", None, "tp"),
            P("blk", None, "tp"),
            P("blk", None, "tp"),
            P("tp", None),
            P("blk"),
            P("blk", None),
            P("blk"),
            P("blk"),
        ),
        out_specs=P("blk", None, "tp"),
        check_vma=False,
    )
```

time: 55.1 us -> 47.9 us (0.87)
  Pallas kernels: 50.3 us -> 45.3 us
  local copies, waits for them, and re-layouts: 2.88 us -> 1.23 us
    pallas_call x1, Pallas kernels: 50.3 us -> 45.3 us  [on_device(): pl.pallas_call(functools.partial(block_kernel, ring=ring), out_shape=pltp...]
    unnamed x1, local copies, waits for them, and re-layouts: 2.88 us -> 1.23 us
where the time goes in v2:
time: 47.9 us; the launch traced here: 47.8 us
  Pallas kernels  45.3 us (95%)
  between operations  1.31 us (3%)
  local copies, waits for them, and re-layouts  1.23 us (3%)
    pallas_call x1, Pallas kernels, on_device(): pl.pallas_call(functools.partial(block_kernel, ring=ring), out_shape=pltp...  45.3 us
    unnamed x1, local copies, waits for them, and re-layouts  1.23 us

profile of v2, /device:TPU:1, one launch (start us, length us, event | category | flops | bytes accessed | tf_op | source)
XLA Modules:
  0.0 47.8 jit_solution(15724702637451106521)
XLA Ops:
  1.3 45.3 %rebalanced_attention.1 = bf16[8,128,896]{2,1,0:T(8,128)(2,1)S(1)} custom-call(s32[4]{0:T(128)} %live_hbm.1, s32[1]{0:T(128)S(6)} %copy.12.left_hbm, s32[1]{0:T(128)S(6)} %copy.13.right_hbm, s32[4,128]{1,0:T(4,128)} %tiles_hbm.1, bf16[4,2048,128]{2,1,0:T(8,128)(2,1)} %k_hbm.1, bf16[4,2048,128]{2,1,0:T(8,128)(2,1)} %v_hbm.1, bf16[4,128,896]{2,1,0:T(8,128)(2,1)} %q_hbm.1, ...), custom_call_target="tpu_custom_call" | custom-call | tf_op jit(solution)/shard_map/rebalanced_attention/pallas_call | solution.py:291
  46.6 1.2 %copy.11 = bf16[8,128,896]{2,1,0:T(8,128)(2,1)} copy(bf16[8,128,896]{2,1,0:T(8,128)(2,1)S(1)} %rebalanced_attention.1) | data formatting | bytes 3670016

commit v3 on v2

--- a/solution.py
+++ b/solution.py
@@ -14,7 +14,7 @@
 MASKED = -(2.0**100)
 MESH = pl.DeviceIdType.MESH
 ORDER = (0, 3, 1, 2)
-GROUPS = ((0, 2), (2, 4), (4, 6), (6, 7))
+GROUPS = ((0, 2), (2, 4), (4, 7))
 PIECES = ((0, 256), (256, 512), (512, 896))
 LAST_PIECES = ((0, 256), (256, 512), (512, 768), (768, 896))
 CHUNK = 512
@@ -28,7 +28,7 @@
     live_hbm, left_hbm, right_hbm, tiles_hbm, k_hbm, v_hbm, q_hbm, hid_hbm, w_hbm,
     out_ref,
     live_ref, left_ref, right_ref, tiles_ref,
-    kb, vb, qb, hb, wb, ind, ones, far, sc, ab, keep, snd, rcv, cut,
+    kb, vb, qb, hb, wb, ind, vt, far, sc, ab, keep, snd, rcv, cut,
     s_sem, k_sem, v_sem, q_sem, h_sem, w_sem, ws_sem, wr_sem, as_sem, ar_sem,
     is_sem, ir_sem, cs_sem, cr_sem,
     *, ring,
@@ -101,7 +101,7 @@
     token = lax.broadcasted_iota(jnp.int32, (tokens, HEAD), 0)
     lane = lax.broadcasted_iota(jnp.int32, (tokens, HEAD), 1)
     ind[...] = jnp.where(token // TILE == lane, 1.0, 0.0).astype(jnp.bfloat16)
-    ones[...] = jnp.ones_like(ones)
+    vt[HEAD:, :] = jnp.ones((16, tokens), jnp.bfloat16)
     zero_rows = jnp.zeros((nodes, width), jnp.bfloat16)
     out_ref[S_MAX] = zero_rows
     out_ref[S_MAX + blocks - 1] = zero_rows
@@ -118,13 +118,15 @@
             copy.start()
 
     scale = jnp.float32(HEAD**-0.5 * math.log2(math.e))
-    attn_copies = [
-        remote(
-            ab.at[j, :, pl.ds(0, width)], ab.at[j, :, pl.ds(width, width)],
-            as_sem.at[j], ar_sem.at[j], partner,
+    swaps = ((0, GROUPS[1][1] * HEAD), (GROUPS[1][1] * HEAD, width))
+    attn_copies = {
+        (j, n): remote(
+            ab.at[j, :, pl.ds(lo, hi - lo)], ab.at[j, :, pl.ds(width + lo, hi - lo)],
+            as_sem.at[j, n], ar_sem.at[j, n], partner,
         )
         for j in range(blocks)
-    ]
+        for n, (lo, hi) in enumerate(swaps)
+    }
     inner = {
         (j, n): remote(
             snd.at[j, :, pl.ds(lo, hi - lo)], rcv.at[j, :, pl.ds(lo, hi - lo)],
@@ -161,32 +163,34 @@
             [qb[j, :, h * HEAD : (h + 1) * HEAD] for h in range(lo, hi)], axis=0
         )
         far_rows = jnp.concatenate([far[j]] * (hi - lo), axis=0)
-        lhs = jnp.concatenate([q_rows, far_rows], axis=1)
-        top = jnp.full((rows, HEAD), -jnp.inf, jnp.float32)
+        rhs = jnp.concatenate([q_rows, far_rows], axis=1)
+        top = jnp.full((8, rows), -jnp.inf, jnp.float32)
         for c in range(0, tokens, CHUNK):
-            rhs = jnp.concatenate([kb[j, c : c + CHUNK, :], ind[c : c + CHUNK, :]], axis=1)
+            lhs = jnp.concatenate([kb[j, c : c + CHUNK, :], ind[c : c + CHUNK, :]], axis=1)
             part = lax.dot_general(
                 lhs, rhs, (((1,), (1,)), ((), ())), preferred_element_type=jnp.float32
             )
-            sc[slot, :rows, c : c + CHUNK] = part
-            for w in range(0, CHUNK, HEAD):
-                top = jnp.maximum(top, part[:, w : w + HEAD])
-        return jnp.max(top, axis=1, keepdims=True)
+            sc[slot, c : c + CHUNK, :rows] = part
+            top = jnp.maximum(top, jnp.max(part.reshape(CHUNK // 8, 8, rows), axis=0))
+        return jnp.max(top, axis=0, keepdims=True)
 
     def mix(j, g, slot, top):
         lo, hi = GROUPS[g]
         rows = (hi - lo) * nodes
         if g == 0:
             v_copies[j].wait()
+            for c in range(0, tokens, HEAD):
+                vt[: HEAD, c : c + HEAD] = jnp.transpose(vb[j, c : c + HEAD, :])
         total = None
         for c in range(0, tokens, CHUNK):
-            part = jnp.exp2((sc[slot, :rows, c : c + CHUNK] - top) * scale).astype(jnp.bfloat16)
-            rhs = jnp.concatenate([vb[j, c : c + CHUNK, :], ones[c : c + CHUNK, :]], axis=1)
-            term = jnp.dot(part, rhs, preferred_element_type=jnp.float32)
+            part = jnp.exp2((sc[slot, c : c + CHUNK, :rows] - top) * scale).astype(jnp.bfloat16)
+            term = jnp.dot(vt[:, c : c + CHUNK], part, preferred_element_type=jnp.float32)
             total = term if total is None else total + term
-        mean = (total[:, :HEAD] / total[:, HEAD:]).astype(jnp.bfloat16)
+        mean = total[:HEAD] / total[HEAD : HEAD + 1]
         for n, h in enumerate(range(lo, hi)):
-            ab[j, :, h * HEAD : (h + 1) * HEAD] = mean[n * nodes : (n + 1) * nodes]
+            ab[j, :, h * HEAD : (h + 1) * HEAD] = jnp.transpose(
+                mean[:, n * nodes : (n + 1) * nodes]
+            ).astype(jnp.bfloat16)
 
     def residual(j, lo, hi, flag):
         rows = hb[j, :, lo:hi].astype(jnp.float32)
@@ -194,19 +198,30 @@
 
     def send_part(n):
         j = ORDER[n]
-        attn_copies[j].wait()
+        for n_swap in range(len(swaps)):
+            attn_copies[j, n_swap].wait()
         move = moved(j)
         pick = half if move is None else half * move + (1 - half) * (1 - move)
+        sums = []
         for p, (lo, hi) in enumerate(pieces_of(j)):
             if n == 0:
                 near_w[p].wait()
                 far_w[p].wait()
-            part = jnp.dot(ab[j], wb[pick, :, lo:hi], preferred_element_type=jnp.float32)
+            sums.append(jnp.dot(ab[j], wb[pick, :, lo:hi], preferred_element_type=jnp.float32))
             if n == 0 and p == 0:
                 hid_copy.wait()
-            part = part + residual(j, lo, hi, None if move is None else move == 1)
-            snd[j, :, lo:hi] = part.astype(jnp.bfloat16)
-            inner[j, p].start()
+            if n == 0:
+                hand_over(j, p, sums[p], move)
+            elif p > 0:
+                hand_over(j, p - 1, sums[p - 1], move)
+        if n > 0:
+            hand_over(j, len(sums) - 1, sums[-1], move)
+
+    def hand_over(j, p, part, move):
+        lo, hi = pieces_of(j)[p]
+        part = part + residual(j, lo, hi, None if move is None else move == 1)
+        snd[j, :, lo:hi] = part.astype(jnp.bfloat16)
+        inner[j, p].start()
 
     def keep_part(n):
         j = ORDER[n]
@@ -237,25 +252,26 @@
                 node < live * (1 - move), total, 0.0
             ).astype(jnp.bfloat16)
 
-    def pass_on(n):
-        attn_copies[ORDER[n]].start()
-        if n == 0:
+    def pass_on(n, part):
+        attn_copies[ORDER[n], part].start()
+        if n == 0 and part == 1:
             far_w[-1].start()
 
     groups = len(GROUPS)
     units = [(j, g) for j in ORDER for g in range(groups)]
     plan = {
-        0: [(enter,)],
-        3: [(pass_on, 0)],
-        4: [(send_part, 0)],
-        7: [(pass_on, 1), (keep_part, 0), (settle, 0, 0)],
-        8: [(settle, 0, 1), (send_part, 1)],
-        9: [(keep_part, 1), (settle, 0, 2)],
-        11: [(pass_on, 2), (settle, 1, 0)],
-        12: [(settle, 1, 1), (send_part, 2)],
-        13: [(keep_part, 2), (settle, 1, 2)],
-        15: [(pass_on, 3), (settle, 2, 0), (send_part, 3), (settle, 2, 1), (keep_part, 3),
-             (settle, 2, 2)] + [(settle, 3, p) for p in range(len(LAST_PIECES))],
+        1: [(pass_on, 0, 0)],
+        2: [(pass_on, 0, 1)],
+        3: [(send_part, 0)],
+        4: [(pass_on, 1, 0)],
+        5: [(pass_on, 1, 1), (keep_part, 0), (settle, 0, 0), (send_part, 1), (settle, 0, 1)],
+        7: [(pass_on, 2, 0), (settle, 0, 2)],
+        8: [(pass_on, 2, 1), (keep_part, 1), (settle, 1, 0), (settle, 1, 1), (send_part, 2)],
+        9: [(settle, 1, 2)],
+        10: [(pass_on, 3, 0)],
+        11: [(pass_on, 3, 1), (keep_part, 2), (settle, 2, 0), (send_part, 3), (settle, 2, 1),
+             (keep_part, 3), (settle, 2, 2)]
+        + [(settle, 3, p) for p in range(len(LAST_PIECES))],
     }
     for copy in small[1:]:
         copy.wait()
@@ -268,6 +284,8 @@
         v_copies[j].start()
     for u, (j, g) in enumerate(units):
         ahead = scores(*units[u + 1], (u + 1) % 2) if u + 1 < len(units) else None
+        if u == 0:
+            enter()
         mix(j, g, u % 2, top)
         top = ahead
         for step, *rest in plan.get(u, ()):
@@ -304,16 +322,16 @@
             pltpu.VMEM((blocks, nodes, width), bf16),
             pltpu.VMEM((2, 2 * width, width), bf16),
             pltpu.VMEM((tokens, HEAD), bf16),
-            pltpu.VMEM((tokens, HEAD), bf16),
+            pltpu.VMEM((HEAD + 16, tokens), bf16),
             pltpu.VMEM((blocks, nodes, HEAD), bf16),
-            pltpu.VMEM((2, rows, tokens), f32),
+            pltpu.VMEM((2, tokens, rows), f32),
             pltpu.VMEM((blocks, nodes, 2 * width), bf16),
             pltpu.VMEM((blocks, nodes, width), f32),
             pltpu.VMEM((blocks, nodes, width), bf16),
             pltpu.VMEM((blocks, nodes, width), bf16),
             pltpu.VMEM((blocks, nodes, width), bf16),
             dma((4,)), dma((blocks,)), dma((blocks,)), dma((blocks,)), dma, dma((parts,)),
-            dma((parts,)), dma((parts,)), dma((blocks,)), dma((blocks,)),
+            dma((parts,)), dma((parts,)), dma((blocks, 2)), dma((blocks, 2)),
             dma((blocks, pieces)), dma((blocks, pieces)),
             dma((blocks, pieces)), dma((blocks, pieces)),
         ],

time: 47.9 us -> 46.8 us (0.977)
  Pallas kernels: 45.3 us -> 44.1 us
    pallas_call x1, Pallas kernels: 45.3 us -> 44.1 us  [on_device(): pl.pallas_call(functools.partial(block_kernel, ring=ring), out_shape=pltp...]
where the time goes in v3:
time: 46.8 us; the launch traced here: 46.6 us
  Pallas kernels  44.1 us (94%)
  between operations  1.31 us (3%)
  local copies, waits for them, and re-layouts  1.23 us (3%)
    pallas_call x1, Pallas kernels, on_device(): pl.pallas_call(functools.partial(block_kernel, ring=ring), out_shape=pltp...  44.1 us
    unnamed x1, local copies, waits for them, and re-layouts  1.23 us

profile of v3, /device:TPU:1, one launch (start us, length us, event | category | flops | bytes accessed | tf_op | source)
XLA Modules:
  0.0 46.6 jit_solution(18013579843372128979)
XLA Ops:
  1.3 44.1 %rebalanced_attention.1 = bf16[8,128,896]{2,1,0:T(8,128)(2,1)S(1)} custom-call(s32[4]{0:T(128)} %live_hbm.1, s32[1]{0:T(128)S(6)} %copy.12.left_hbm, s32[1]{0:T(128)S(6)} %copy.13.right_hbm, s32[4,128]{1,0:T(4,128)} %tiles_hbm.1, bf16[4,2048,128]{2,1,0:T(8,128)(2,1)} %k_hbm.1, bf16[4,2048,128]{2,1,0:T(8,128)(2,1)} %v_hbm.1, bf16[4,128,896]{2,1,0:T(8,128)(2,1)} %q_hbm.1, ...), custom_call_target="tpu_custom_call" | custom-call | tf_op jit(solution)/shard_map/rebalanced_attention/pallas_call | solution.py:309
  45.4 1.2 %copy.11 = bf16[8,128,896]{2,1,0:T(8,128)(2,1)} copy(bf16[8,128,896]{2,1,0:T(8,128)(2,1)S(1)} %rebalanced_attention.1) | data formatting | bytes 3670016
